TPU v7x, 16 devices: a 4x2x1 block of a 4x4x8 slice. The times are simulated.
16 devices in a mesh: seqs: 2 (over y, z), states: 8 (over x, core).
Axes of the slice: x: 4, y: 2, z: 1, core: 2. Of those that a mesh axis runs over, the one named last changes fastest.
The devices are a block of a 4x4x8 slice.
Arguments:
- trans_mat: bfloat16 [16384, 16384], P(None, 'states')
- emit_mat: bfloat16 [16384, 10000], P('states')
- init_prob: float32 [16384], P('states')
- tokens: int32 [256, 16], P('seqs'), parts along dimension 0
- lengths: int32 [256], P('seqs'), parts along dimension 0
Outputs:
- output 1: float32 [256], P('seqs'), parts along dimension 0
- output 2: float32 [256, 16384], P('seqs', 'states'), parts along dimension 0
- output 3: float32 [32768, 2048], P(('seqs', 'states')), parts along dimension 0
There are 2 independent parts. A program takes and returns all parts, laid end to end along the dimension named above; an argument that names none is the same for every part.
All inputs are finite; a program needn't handle non-finite values.
Results may differ from a plain program's by a relative error of at most 0.001.
Values are sent between devices in bfloat16 or wider.
A program may use at most 768 MiB of HBM per device.

v0:
```python
import functools

import jax
import jax.numpy as jnp
from jax import lax
from jax.experimental import pallas as pl
from jax.experimental.pallas import tpu as pltpu
from jax.sharding import PartitionSpec as P

MESH = pl.DeviceIdType.MESH
ANY = pl.BlockSpec(memory_space=pl.ANY)
VMEM = pl.BlockSpec(memory_space=pltpu.VMEM)
LANES = 128
BOTH = (0, 1)
VMEM_BYTES = 67043328


def _place(n):
    me = lax.axis_index('states')
    core = lax.rem(me, 2)
    chip = lax.div(me, 2)
    partner = chip * 2 + (1 - core)
    right = lax.rem(me + 2, n)
    left = lax.rem(me + n - 2, n)
    return me, chip, core, partner, right, left


def _dev(peer):
    return {'states': peer}


def _arrive(me, n):
    for r in range(1, n):
        pl.semaphore_signal(pltpu.get_barrier_semaphore(), inc=1, device_id=_dev(lax.rem(me + r, n)), device_id_type=MESH)


def _all_here(n):
    pl.semaphore_wait(pltpu.get_barrier_semaphore(), n - 1)


def _remote(src, dst, ssem, rsem, peer):
    return pltpu.make_async_remote_copy(src_ref=src, dst_ref=dst, send_sem=ssem, recv_sem=rsem, device_id=_dev(peer), device_id_type=MESH)


def _spans(width, size=LANES):
    return [slice(o, o + size) for o in range(0, width, size)]


def _dot(x, y):
    return jnp.dot(x, y, preferred_element_type=jnp.float32)


def _fwd_kernel(n, steps, rows, nbuf, a_hbm, e_hbm, pi_ref, code_ref, sid_ref, info_ref, al_hbm, a0_hbm, x_hbm, at_hbm, cc_ref, ll_ref,
                g, w, u, al, ebuf, a0b, xi, fs, fr, ta, tt, safe_ref, lacc, tbuf, cs_send, cs_recv,
                e_sem, w_sem, r_sem, out_sem, ta_sem, tt_sem, cs_ss, cs_rs, ici_ss, ici_rs, dd_ss, dd_rs):
    me, chip, core, partner, right, left = _place(n)
    chips = n // 2
    wide = al.shape[1]
    part_w = wide // 4
    seqs = a0b.shape[0]
    a0f = u.at[pl.ds(0, seqs), :]
    quarters = range(4)
    per_step = 2 * 8
    total = (steps - 1) * per_step

    def quarter(j, cls, i):
        far = lax.rem(j + 2 + 2 * i, 4)
        qq = jnp.where(j < 2, 2 * j + i, far)
        off = jnp.where(j < 2, 0, jnp.where(j >= 6, 2, jnp.where(i == 0, chips - 1, 1)))
        c = lax.rem(chip + off, chips)
        k = jnp.where(cls == 0, core, 1 - core)
        return (c * 2 + k) * 4 + qq

    def a_part(b):
        return a_hbm.at[pl.ds(pl.multiple_of(b * part_w, part_w), part_w), :]

    def stream(q, slot):
        k = lax.rem(q, per_step)
        return pltpu.make_async_copy(a_part(quarter(lax.div(k, 2), 1, lax.rem(k, 2))), w.at[per_step + slot], w_sem.at[slot])

    def resident(j, i):
        return pltpu.make_async_copy(a_part(quarter(j, 0, i)), w.at[2 * j + i], r_sem.at[2 * j + i])

    def e_rows(first, count, dst, sem):
        return pltpu.make_async_copy(e_hbm.at[pl.ds(pl.multiple_of(first, 8), count), :], dst, sem)

    def e_copy(s):
        return e_rows((s - 1) * rows, rows, ebuf.at[lax.rem(s, 2)], e_sem.at[lax.rem(s, 2)])

    def al_copy(s):
        return pltpu.make_async_copy(al, al_hbm.at[s], out_sem.at[4])

    def mine(b):
        return g.at[b, pl.ds(0, rows), :]

    def x_copy(s, q):
        return pltpu.make_async_copy(mine(me * 4 + q), x_hbm.at[s, :, pl.ds(q * part_w, part_w)], out_sem.at[q])

    pieces, depth, size = at_hbm.shape[0], ta.shape[0], ta.shape[1]

    def ta_copy(c):
        slot = lax.rem(c, depth)
        return pltpu.make_async_copy(a_hbm.at[pl.ds(pl.multiple_of(c * size, size), size), :], ta.at[slot], ta_sem.at[slot])

    def tt_copy(c):
        slot = lax.rem(c, depth)
        return pltpu.make_async_copy(tt.at[slot], at_hbm.at[c], tt_sem.at[slot])

    def turn(s):
        def one(c, _):
            ta_copy(c).wait()

            @pl.when(c >= depth)
            def _():
                tt_copy(c - depth).wait()

            slot = lax.rem(c, depth)
            tt[slot] = ta[slot].T
            tt_copy(c).start()

            @pl.when(c + depth < pieces)
            def _():
                ta_copy(c + depth).start()

            return 0

        lax.fori_loop(lax.div((s - 1) * pieces, steps - 1), lax.div(s * pieces, steps - 1), one, 0)

    e0_copy = e_rows((steps - 1) * rows, seqs, a0b, e_sem.at[0])
    e0_copy.start()
    _arrive(me, n)

    def load(j, _):
        for i in BOTH:
            resident(j, i).start()
        return 0

    for c in range(depth):
        ta_copy(jnp.int32(c)).start()
    for q in range(nbuf):
        stream(jnp.int32(q), q).start()
    lax.fori_loop(0, 2, load, 0)
    e_copy(jnp.int32(1)).start()
    tbuf[...] = jnp.zeros_like(tbuf)
    lacc[...] = jnp.zeros_like(lacc)
    if g.shape[1] > rows:
        pad = jnp.zeros((g.shape[1] - rows, part_w), jnp.bfloat16)

        def clear(k, _):
            g[k, rows:, :] = pad
            return 0

        lax.fori_loop(0, 4 * n, clear, 0)

    def ici(k, src, dst, i):
        return _remote(src, dst, ici_ss.at[k], ici_rs.at[k], left if i else right)

    def early(i):
        return ici(i, fs.at[i], fr.at[i], i)

    def own_ring(j, i):
        b = me * 4 + (j + 2 + 2 * i) % 4
        return ici(2 * (j - 2) + i, mine(b), mine(b), i)

    def relay(j, i):
        b = quarter(j, 0, i)
        return ici(2 * (j + 2) + i, mine(b), mine(b), i)

    def dd(j, cls, i):
        b = quarter(j, cls, i)
        return _remote(mine(b), mine(b), dd_ss.at[2 * j + i], dd_rs.at[2 * j + i], partner)

    lane = lax.broadcasted_iota(jnp.int32, (rows, seqs), 1).astype(jnp.float32)
    row = lax.broadcasted_iota(jnp.int32, (rows, seqs), 0).astype(jnp.float32)

    def starting(s):
        return sid_ref[s, 0:rows, :].astype(jnp.float32)

    def first_alphas(s):
        pick = (starting(s) == lane).astype(jnp.bfloat16)
        xi[...] = _dot(pick, a0b[...]).astype(jnp.bfloat16)

    def normalizer(part, count, meanwhile):
        tbuf[0:count, :] = part
        row = jnp.sum(tbuf[...].T, axis=0, keepdims=True)
        cs_send[...] = jnp.broadcast_to(row, cs_send.shape)
        cs_recv[me] = jnp.broadcast_to(row, cs_send.shape)
        cps = []
        for r in sorted(range(1, n), key=lambda r: abs(2 * r - n)):
            cp = _remote(cs_send, cs_recv.at[me], cs_ss.at[r - 1], cs_rs.at[r - 1], lax.rem(me + r, n))
            cp.start()
            cps.append(cp)
        meanwhile()
        for cp in cps:
            cp.wait()
        crow = cs_recv[0]
        for r in range(1, n):
            crow = crow + cs_recv[r]
        return crow, jnp.broadcast_to(crow[0:1, :], (LANES, LANES)).T[0:count, :]

    def add_log(s, ccol):
        slot, begin, end = info_ref[0:1, :], info_ref[1:2, :], info_ref[2:3, :]
        now = jnp.full((rows, seqs), s, jnp.int32).astype(jnp.float32)
        here = (slot == row) & (now > begin) & (now <= end)
        lacc[...] += jnp.where(here, jnp.log(jnp.where(here, ccol, 1.0)), 0.0)

    def exchange(s, then):
        own = [own_ring(3, i) for i in BOTH] + [dd(j, 0, i) for j in BOTH for i in BOTH]
        own += [own_ring(j, i) for j in (4, 5) for i in BOTH]
        for cp in own:
            cp.start()
        then()

        def arrived(j):
            for i in BOTH:
                b = quarter(j, 0, i)
                ici(2 * (j - 2) + i, mine(b), mine(b), i).wait_recv()

        def pass_on(j):
            for i in BOTH:
                dd(j, 0, i).start()

        def rounds(h, _):
            j, k = 2 * h, 2 * h + 1

            @pl.when(h == 1)
            def _():
                for i in BOTH:
                    early(i).wait_recv()
                safe = safe_ref[...]
                for i in BOTH:
                    b = quarter(2, 0, i)
                    for cols in _spans(part_w):
                        g[b, 0:rows, cols] = (fr[i, :, cols] / safe).astype(jnp.bfloat16)
                    relay(2, i).start()
                pass_on(2)

            @pl.when((h == 2) & (s + 2 < steps))
            def _():
                first_alphas(s + 1)

            @pl.when(s == 0)
            def _():
                for r in (j, k):
                    for i in BOTH:
                        resident(r, i).wait()

                    @pl.when(h < 2)
                    def _():
                        load(r + 4, 0)

            @pl.when(h >= 2)
            def _():
                arrived(j)
                pass_on(j)

            def own_class(r):
                return sum(_dot(g[quarter(r, 0, i)], w[2 * r + i]) for i in BOTH)

            def other_class(r):
                q = s * per_step + 2 * r
                slots = [lax.rem(q + i, nbuf) for i in BOTH]
                for i in BOTH:
                    dd(r, 1, i).wait_recv()
                    stream(q + i, slots[i]).wait()
                out = sum(_dot(g[quarter(r, 1, i)], w[per_step + slots[i]]) for i in BOTH)

                for i in BOTH:
                    @pl.when(q + i + nbuf < total)
                    def _():
                        stream(q + i + nbuf, slots[i]).start()

                return out

            prod = own_class(j)

            @pl.when(h >= 1)
            def _():
                arrived(k)

            @pl.when(h == 1)
            def _():
                for i in BOTH:
                    relay(3, i).start()

            @pl.when(h >= 1)
            def _():
                pass_on(k)

            u[...] += prod + own_class(k)
            u[...] += other_class(j)
            u[...] += other_class(k)
            return 0

        lax.fori_loop(0, 4, rounds, 0)
        for i in BOTH:
            early(i).wait_send()
            for j in (2, 3):
                relay(j, i).wait_send()
            for j in range(2, 8):
                dd(j, 0, i).wait_send()
        for cp in own:
            cp.wait_send()

    def keep(s):
        for q in quarters:
            x_copy(s, q).start()

    e0_copy.wait()
    def lanes(q):
        return pl.ds(pl.multiple_of(q * LANES, LANES), LANES)

    def first_mass(q, part):
        a = jnp.broadcast_to(pi_ref[:, lanes(q)], (seqs, LANES)) * a0b[:, lanes(q)].astype(jnp.float32)
        a0f[:, lanes(q)] = a
        return part + a

    part = lax.fori_loop(0, wide // LANES, first_mass, jnp.zeros((seqs, LANES), jnp.float32))
    _all_here(n)

    c0_row, c0 = normalizer(part, seqs, lambda: lax.fori_loop(2, 4, load, 0))
    ll_ref[...] = jnp.log(c0_row)

    def first_alpha(q, _):
        alpha = a0f[:, lanes(q)] / c0
        a0f[:, lanes(q)] = alpha
        a0b[:, lanes(q)] = alpha.astype(jnp.bfloat16)
        return 0

    lax.fori_loop(0, wide // LANES, first_alpha, 0)
    a0_copy = pltpu.make_async_copy(a0f, a0_hbm, e_sem.at[0])
    a0_copy.start()
    first_alphas(0)
    for q, cols in enumerate(_spans(wide, part_w)):
        g[me * 4 + q, 0:rows, :] = xi[:, cols]
    safe_ref[...] = jnp.ones_like(safe_ref)
    for i in BOTH:
        fs[i] = xi[:, 2 * i * part_w:(2 * i + 1) * part_w].astype(jnp.float32)
        early(i).start()
    tbuf[...] = jnp.zeros_like(tbuf)
    a0_copy.wait()
    u[...] = jnp.zeros_like(u)

    def step(s, _):
        exchange(s - 1, lambda: keep(s - 1))
        e_copy(s).wait()

        @pl.when(s + 1 < steps)
        def _():
            e_copy(s + 1).start()

        @pl.when(s > 1)
        def _():
            al_copy(s - 1).wait()

        part = jnp.zeros((rows, LANES), jnp.float32)
        eb = ebuf.at[lax.rem(s, 2)]
        for cols in _spans(wide):
            a = u[0:rows, cols] * eb[:, cols].astype(jnp.float32)
            al[:, cols] = a
            part = part + a
        live = code_ref[s, 0:rows, :].astype(jnp.float32) > 0.5
        starts = starting(s) > -0.5

        def meanwhile():
            @pl.when(s + 1 < steps)
            def _():
                for i in BOTH:
                    for cols in _spans(part_w):
                        from_col = 2 * i * part_w + cols.start
                        src = slice(from_col, from_col + LANES)
                        v = jnp.where(live, al[:, src], 0.0)
                        fs[i, :, cols] = jnp.where(starts, xi[:, src].astype(jnp.float32), v)
                    early(i).start()

            turn(s)
            u[...] = jnp.zeros_like(u)

            @pl.when(s > 1)
            def _():
                add_log(s - 1, cc_ref[s - 1])

            for q in quarters:
                x_copy(s - 1, q).wait()

        _, ccol = normalizer(part, rows, meanwhile)
        cc_ref[s] = ccol
        safe = jnp.where(live, ccol, 1.0)
        safe_ref[...] = jnp.where(starts, 1.0, safe)
        for q, block in enumerate(_spans(wide, part_w)):
            for cols in _spans(part_w):
                src = slice(block.start + cols.start, block.start + cols.stop)
                alpha = jnp.where(live, al[:, src] / safe, 0.0)
                al[:, src] = alpha
                x = jnp.where(starts, xi[:, src].astype(jnp.float32), alpha)
                g[me * 4 + q, 0:rows, cols] = x.astype(jnp.bfloat16)

        al_copy(s).start()
        return 0

    lax.fori_loop(1, steps, step, 0)
    add_log(steps - 1, cc_ref[steps - 1])
    ll_ref[...] += jnp.sum(lacc[...], axis=0, keepdims=True)
    al_copy(steps - 1).wait()
    for c in range(depth):
        tt_copy(pieces - depth + c).wait()


def _forward(n, cid, rows, a_loc, e_rows, init_loc, code, sid, info):
    wide = a_loc.shape[1]
    steps, seqs, _ = code.shape
    part_w = wide // 4
    full = max(LANES, rows)
    nbuf = 6 if rows <= 80 else 4
    f32, bf16 = jnp.float32, jnp.bfloat16
    dma = pltpu.SemaphoreType.DMA
    return pl.pallas_call(
        functools.partial(_fwd_kernel, n, steps, rows, nbuf),
        out_shape=(
            jax.ShapeDtypeStruct((steps, rows, wide), f32),
            jax.ShapeDtypeStruct((seqs, wide), f32),
            jax.ShapeDtypeStruct((steps - 1, rows, wide), bf16),
            jax.ShapeDtypeStruct((2 * a_loc.shape[0] // part_w, wide, part_w // 2), bf16),
            jax.ShapeDtypeStruct((steps, rows, LANES), f32),
            jax.ShapeDtypeStruct((8, LANES), f32),
        ),
        in_specs=[ANY, ANY, VMEM, VMEM, VMEM, VMEM],
        out_specs=(ANY, ANY, ANY, ANY, VMEM, VMEM),
        scratch_shapes=[
            pltpu.VMEM((4 * n, full, part_w), bf16),
            pltpu.VMEM((2 * n + nbuf, part_w, wide), bf16),
            pltpu.VMEM((full, wide), f32),
            pltpu.VMEM((rows, wide), f32),
            pltpu.VMEM((2, rows, wide), bf16),
            pltpu.VMEM((seqs, wide), bf16),
            pltpu.VMEM((rows, wide), bf16),
            pltpu.VMEM((2, rows, part_w), f32),
            pltpu.VMEM((2, rows, part_w), f32),
            pltpu.VMEM((4, part_w // 2, wide), bf16),
            pltpu.VMEM((4, wide, part_w // 2), bf16),
            pltpu.VMEM((rows, LANES), f32),
            pltpu.VMEM((rows, LANES), f32),
            pltpu.VMEM((LANES, LANES), f32),
            pltpu.VMEM((8, LANES), f32),
            pltpu.VMEM((n, 8, LANES), f32),
            dma((2,)), dma((nbuf,)), dma((2 * n,)), dma((5,)), dma((4,)), dma((4,)),
            dma((n - 1,)), dma((n - 1,)),
            dma((12,)), dma((12,)), dma((2 * n,)), dma((2 * n,)),
        ],
        compiler_params=pltpu.CompilerParams(collective_id=cid, has_side_effects=True, vmem_limit_bytes=VMEM_BYTES),
        name='forward',
    )(a_loc, e_rows, init_loc, code, sid, info)


def _bwd_kernel(n, steps, rows, nbuf, at_hbm, e_hbm, cc_ref, code_ref, w_hbm,
                w, wv, ebuf, pp, rp, rs, rin,
                e_sem, w_sem, r_sem, out_sem, dd_ss, dd_rs, ici_ss, ici_rs):
    me, chip, core, partner, right, left = _place(n)
    chips = n // 2
    wide = wv.shape[1]
    size = at_hbm.shape[2]
    per = wide // size // 2
    trips = steps - 2
    rounds_n = 4 * per
    count = 2 * rounds_n
    ringed = 6 * per
    total = trips * rounds_n

    def piece(j, cls, i):
        p, e = lax.div(j, per), lax.rem(j, per)
        hh = jnp.where(p == 1, 1 - i, i)
        off = jnp.where(p == 0, 2, jnp.where(p == 3, 0, chips - 1 if i else 1))
        c = lax.rem(chip + off, chips)
        k = 1 - core if cls else core
        return (c * 2 + k) * 2 * per + hh * per + e

    def fetch(j, cls, i, slot, sem):
        return pltpu.make_async_copy(at_hbm.at[piece(j, cls, i)], w.at[slot, :, pl.ds(i * size, size)], sem)

    def stream(j, i, slot):
        return fetch(j, 1, i, rounds_n + slot, w_sem.at[slot, i])

    def resident(j, i):
        return fetch(j, 0, i, j, r_sem.at[j, i])

    def e_copy(t):
        first = pl.multiple_of((steps - 2 - t) * rows, 8)
        return pltpu.make_async_copy(e_hbm.at[pl.ds(first, rows), :], ebuf.at[lax.rem(t, 2)], e_sem.at[lax.rem(t, 2)])

    def w_copy(t):
        return pltpu.make_async_copy(wv.at[pl.ds(0, rows), :], w_hbm.at[steps - 2 - t], out_sem)

    for t in BOTH:
        e_copy(jnp.int32(t)).start()
    _arrive(me, n)

    def load(j, _):
        for i in BOTH:
            resident(j, i).start()
        return 0

    for q in BOTH:
        for i in BOTH:
            stream(jnp.int32(q), i, q).start()
        load(jnp.int32(q), 0)
    if wv.shape[0] > rows:
        wv[rows:, :] = jnp.zeros((wv.shape[0] - rows, wide), jnp.bfloat16)

    def dd(k):
        return _remote(pp.at[k], rp.at[k], dd_ss.at[k], dd_rs.at[k], partner)

    def ring(k, par, i):
        return _remote(rs.at[k], rin.at[par, k], ici_ss.at[k], ici_rs.at[par, k], left if i else right)

    def weigh(s, eb, o, beta):
        code = code_ref[s, 0:rows, :].astype(jnp.float32)
        ok = code > 2.5
        safe = jnp.where(ok, cc_ref[s], 1.0)
        for cols in _spans(size):
            dst = slice(o + cols.start, o + cols.stop)
            b = 1.0 if beta is None else jnp.where(code > 3.5, 1.0, beta[:, cols])
            v = eb[:, dst].astype(jnp.float32) * b / safe
            wv[0:rows, dst] = jnp.where(ok, v, 0.0).astype(jnp.bfloat16)

    e_copy(jnp.int32(0)).wait()
    for cols in _spans(wide, size):
        weigh(steps - 1, ebuf.at[0], cols.start, None)
    ahead = 4
    for q in range(2, nbuf):
        for i in BOTH:
            stream(jnp.int32(q), i, q).start()
    for q in range(2, ahead):
        load(jnp.int32(q), 0)
    w_copy(jnp.int32(0)).start()
    _all_here(n)

    def step(t, _):
        par = lax.rem(t, 2)

        def finish(j):
            p = lax.div(j, per)
            for i in BOTH:
                dd(2 * j + i).wait_recv()

            @pl.when(p == 2)
            def _():
                for i in BOTH:
                    k = 2 * j + i
                    c = k - 4 * per
                    ring(c, par, i).wait_recv()
                    rp[k] += rin[par, c]

            for i in BOTH:
                k = 2 * j + i
                rs[k] += rp[k]

            @pl.when(p < 3)
            def _():
                for i in BOTH:
                    ring(2 * j + i, par, i).start()

        def rounds(j, _):
            q = t * rounds_n + j
            slot = lax.rem(q, nbuf)
            for i in BOTH:
                stream(j, i, slot).wait()
            prod = _dot(wv[...], w[rounds_n + slot])
            for i, cols in enumerate(_spans(2 * size, size)):
                k = 2 * j + i
                pp[k] = prod[0:rows, cols]
                dd(k).start()

            @pl.when(q + nbuf < total)
            def _():
                for i in BOTH:
                    stream(lax.rem(j + nbuf, rounds_n), i, slot).start()

            @pl.when(j > 0)
            def _():
                finish(j - 1)

            @pl.when(t == 0)
            def _():
                for i in BOTH:
                    resident(j, i).wait()

                @pl.when(j < rounds_n - ahead)
                def _():
                    load(j + ahead, 0)

            prod = _dot(wv[...], w[j])
            for i, cols in enumerate(_spans(2 * size, size)):
                rs[2 * j + i] = prod[0:rows, cols]
            return 0

        lax.fori_loop(0, rounds_n, rounds, 0)
        finish(jnp.int32(rounds_n - 1))

        def gone(k, _):
            dd(k).wait_send()
            return 0

        def sent(k, _):
            ring(k, par, 0).wait_send()
            return 0

        lax.fori_loop(0, count, gone, 0)
        lax.fori_loop(0, 4 * per, sent, 0)
        nxt = t + 1
        e_copy(nxt).wait()

        @pl.when(nxt + 1 < steps - 1)
        def _():
            e_copy(nxt + 1).start()

        w_copy(t).wait()
        eb = ebuf.at[lax.rem(nxt, 2)]
        for e in range(per):
            for i in BOTH:
                near, late = 2 * (per + e) + 1 - i, 2 * (2 * per + e) + i
                ring(near, par, 1 - i).wait_recv()
                ring(late, par, i).wait_recv()
                beta = rs[ringed + 2 * e + i] + rin[par, near] + rin[par, late]
                weigh(steps - 1 - nxt, eb, (i * per + e) * size, beta)
        w_copy(nxt).start()
        lax.fori_loop(4 * per, ringed, sent, 0)
        return 0

    lax.fori_loop(0, trips, step, 0)
    w_copy(jnp.int32(trips)).wait()


def _backward(n, cid, at_loc, e_rows, ccol, code):
    pieces, wide, size = at_loc.shape
    steps, rows, _ = ccol.shape
    full = max(LANES, rows)
    count = pieces // 2
    nbuf = 6 if rows <= 80 else 4
    ringed = 3 * count // 4
    f32, bf16 = jnp.float32, jnp.bfloat16
    dma = pltpu.SemaphoreType.DMA
    return pl.pallas_call(
        functools.partial(_bwd_kernel, n, steps, rows, nbuf),
        out_shape=jax.ShapeDtypeStruct((steps - 1, rows, wide), bf16),
        in_specs=[ANY, ANY, VMEM, VMEM],
        out_specs=ANY,
        scratch_shapes=[
            pltpu.VMEM((count // 2 + nbuf, wide, 2 * size), bf16),
            pltpu.VMEM((full, wide), bf16),
            pltpu.VMEM((2, rows, wide), bf16),
            pltpu.VMEM((count, rows, size), f32),
            pltpu.VMEM((count, rows, size), f32),
            pltpu.VMEM((count, rows, size), f32),
            pltpu.VMEM((2, ringed, rows, size), f32),
            dma((2,)), dma((nbuf, 2)), dma((count // 2, 2)), dma(()),
            dma((count,)), dma((count,)),
            dma((ringed,)), dma((2, ringed)),
        ],
        compiler_params=pltpu.CompilerParams(collective_id=cid, has_side_effects=True, vmem_limit_bytes=VMEM_BYTES),
        name='backward',
    )(at_loc, e_rows, ccol, code)


def _pair_kernel(group_ref, a_ref, x_ref, w_ref, o_ref):
    pair_sum = lax.dot_general(x_ref[...], w_ref[...], (((0,), (0,)), ((), ())), preferred_element_type=jnp.float32)
    o_ref[...] = a_ref[...].astype(jnp.float32) * pair_sum


def _pairs(group, a_loc, xs, ws):
    depth, wide = ws.shape
    size = wide // 8
    tiles = wide // size
    return pl.pallas_call(
        _pair_kernel,
        out_shape=jax.ShapeDtypeStruct((wide, wide), jnp.float32),
        grid_spec=pltpu.PrefetchScalarGridSpec(
            num_scalar_prefetch=1,
            grid=(tiles,),
            in_specs=[
                pl.BlockSpec((size, wide), lambda i, group_ref: (group_ref[0] * tiles + i, 0)),
                pl.BlockSpec((depth, size), lambda i, group_ref: (0, i)),
                pl.BlockSpec((depth, wide), lambda i, group_ref: (0, 0)),
            ],
            out_specs=pl.BlockSpec((size, wide), lambda i, group_ref: (i, 0)),
        ),
        compiler_params=pltpu.CompilerParams(vmem_limit_bytes=VMEM_BYTES),
        name='pairs',
    )(group, a_loc, xs, ws)


def _plan_kernel(options, len_ref, tok_ref, code_ref, sid_ref, look_ref, info_ref, pick_ref):
    seqs = len_ref.shape[1]
    steps = tok_ref.shape[0]
    f32, bf16 = jnp.float32, jnp.bfloat16
    square = (seqs, seqs)
    up = lax.broadcasted_iota(jnp.int32, square, 0).astype(f32)
    across = lax.broadcasted_iota(jnp.int32, square, 1).astype(f32)

    def spread(row):
        return jnp.broadcast_to(row, square)

    def total(x):
        return jnp.sum(x, axis=0, keepdims=True)

    length = len_ref[...].astype(f32)
    l_row = spread(length)
    l_col = l_row.T
    ahead = (l_col > l_row) | ((l_col == l_row) & (up < across))
    rank = total(jnp.where(ahead, 1.0, 0.0))
    rank_col = spread(rank).T

    def mates(slots):
        slot = jnp.where(rank < slots, rank, 2 * slots - 1 - rank)
        return slot, total(jnp.where(rank_col == spread(slot), l_col, 0.0))

    slots = jnp.full((1, 1), seqs, jnp.int32).astype(f32)
    pick = jnp.full((1, 1), len(options) - 1, jnp.int32)
    for k in reversed(range(len(options) - 1)):
        _, first = mates(options[k])
        worst = jnp.max(jnp.where(rank < options[k], 0.0, first + length), axis=1, keepdims=True)
        fits = worst <= steps + 1
        slots = jnp.where(fits, options[k], slots)
        pick = jnp.where(fits, k, pick)
    pick_ref[...] = pick
    slot, first = mates(slots)
    opens = rank < slots
    begin = jnp.where(opens, 0.0, first - 1)
    end = begin + length - 1
    info_ref[0:1, :] = slot
    info_ref[1:2, :] = begin
    info_ref[2:3, :] = end
    info_ref[3:4, :] = end * slots + slot

    double = total(jnp.where((spread(slot).T == spread(slot)) & (up != across), 1.0, 0.0))
    shadowed = opens & (length < 1.5) & (double > 0.5)
    home = (spread(slot) == up).astype(bf16)
    slot_col, begin_col, end_col = spread(slot).T, spread(begin).T, spread(end).T
    hidden_col = spread(jnp.where(shadowed, 1.0, 0.0)).T

    for s in range(steps):
        moves = (begin_col < s) & (end_col >= s)
        kind = jnp.where(moves, jnp.where(end_col == s, 4.0, 3.0), 0.0)
        code_ref[s] = _dot(home, kind.astype(bf16)).astype(bf16)
        number = jnp.where((begin_col == s) & (hidden_col < 0.5), up + 1, 0.0)
        sid_ref[s] = (_dot(home, number.astype(bf16)) - 1).astype(bf16)
    away = (slot_col == across).astype(bf16)
    shape = (steps, seqs)
    pos = lax.broadcasted_iota(jnp.int32, shape, 0).astype(f32) - jnp.broadcast_to(begin, shape)
    tok = jnp.zeros(shape, f32)
    for t in range(1, steps):
        there = (pos == t) & (jnp.broadcast_to(length, shape) > t)
        tok = tok + jnp.where(there, jnp.broadcast_to(tok_ref[t:t + 1, :].astype(f32), shape), 0.0)
    high = jnp.floor(tok / LANES)
    low = tok - high * LANES
    look = _dot(high.astype(bf16), away) * LANES + _dot(low.astype(bf16), away)
    look_ref[...] = look.astype(jnp.int32)


def _plan(options, lengths, tokens):
    steps, seqs = tokens.shape
    bf16 = jnp.bfloat16
    return pl.pallas_call(
        functools.partial(_plan_kernel, options),
        out_shape=(
            jax.ShapeDtypeStruct((steps, seqs, LANES), bf16),
            jax.ShapeDtypeStruct((steps, seqs, LANES), bf16),
            jax.ShapeDtypeStruct((steps, seqs), jnp.int32),
            jax.ShapeDtypeStruct((8, seqs), jnp.float32),
            jax.ShapeDtypeStruct((1, 1), jnp.int32),
        ),
        in_specs=[VMEM, VMEM],
        out_specs=(VMEM, VMEM, VMEM, VMEM, VMEM),
        name='plan',
    )(lengths[None, :], tokens)


def solution(mesh):
    n = mesh.shape['states']

    def local_run(trans_loc, emit_loc, init_loc, tokens_loc, lengths_loc):
        seqs, steps = tokens_loc.shape
        wide = trans_loc.shape[1]
        group = lax.axis_index('states').astype(jnp.int32)[None]
        options = (seqs * 9 // 16, seqs * 5 // 8, seqs)
        code, sid, look, info, pick = _plan(options, lengths_loc, tokens_loc.T)

        def run(k):
            rows = options[k]
            tokens = jnp.concatenate([look[1:, 0:rows].reshape(-1), tokens_loc[:, 0]])
            e_rows = jnp.take(emit_loc, tokens, axis=1, mode='clip').T
            al, a0, xs, at_loc, ccol, ll = _forward(n, 2 * k, rows, trans_loc, e_rows, init_loc[None, :], code, sid, info)
            ws = _backward(n, 2 * k + 1, at_loc, e_rows, ccol, code)
            counts = _pairs(group, trans_loc, xs.reshape(-1, wide), ws.reshape(-1, wide))
            last = jnp.take(al.reshape(steps * rows, wide), info[3].astype(jnp.int32), axis=0, mode='clip')
            return ll[0], jnp.where((lengths_loc == 1)[:, None], a0, last), counts

        return lax.switch(pick[0, 0], [functools.partial(run, k) for k in range(len(options))])

    return jax.shard_map(local_run, mesh=mesh, in_specs=(P(None, 'states'), P('states', None), P('states'), P('seqs', None), P('seqs')), out_specs=(P('seqs'), P('seqs', 'states'), P(('seqs', 'states'), None)), check_vma=False)
```

profile of v0, /device:TPU:112, one launch (start us, length us, event | category | flops | bytes accessed | tf_op | source)
XLA Modules:
  0.0 649.8 jit_solution(14244574244523814293)
XLA Ops:
  0.6 2.6 plan.1
  3.9 646.0 %conditional.1 = (f32[128]{0:T(128)}, f32[128,2048]{1,0:T(8,128)}, f32[2048,2048]{1,0:T(8,128)}) conditional(s32[]{:T(128)} %bitcast.27, (s32[16,128]{1,0:T(8,128)S(1)}, s32[128,16]{0,1:T(8,128)}, bf16[2048,10000]{0,1:T(8,128)(2,1)}, f32[2048]{0:T(1024)}, bf16[16384,2048]{1,0:T(8,128)(2,1)}, ...), branch_computations={%region_0.1_spmd, %region_1.2_spmd, %region_2.3_spmd} | conditional | flops 267520 | bytes 26265424 | solution.py:797
  3.9 0.7 slice_bitcast_fusion.1
  4.6 0.1 reshape.69
  4.6 0.1 pad_add_fusion
  4.7 17.4 %gather_fusion = bf16[1208,2048]{1,0:T(8,128)(2,1)} fusion(bf16[2048,10000]{0,1:T(8,128)(2,1)} %get-tuple-element.136, s32[2048]{0:T(1024)S(1)} %pad_clamp_fusion), kind=kCustom, calls=%fused_computation | custom fusion | bytes 9900768 | tf_op jit(solution)/shard_map/cond/branch_0_fun/jit(_take)/gather | solution.py:790
  22.2 266.8 %forward.3 = (f32[16,72,2048]{2,1,0:T(8,128)}, f32[128,2048]{1,0:T(8,128)}, bf16[15,72,2048]{2,1,0:T(8,128)(2,1)}, bf16[64,2048,256]{2,1,0:T(8,128)(2,1)}, f32[16,72,128]{2,1,0:T(8,128)}, /*index=5*/f32[8,128]{1,0:T(8,128)}) custom-call(bf16[16384,2048]{1,0:T(8,128)(2,1)} %get-tuple-element.142.a_hbm.a_ref, bf16[1208,2048]{1,0:T(8,128)(2,1)} %gather_fusion, ...), custom_call_target="tpu_custom_call" | custom-call | tf_op jit(solution)/shard_map/cond/branch_0_fun/forward/pallas_call | solution.py:417
  288.9 0.0 copy-start.3
  289.0 0.0 copy-start
  289.0 1.3 slice_bitcast_fusion
  290.2 0.7 convert_bitcast_fusion
  290.9 5.1 gather_fusion.1
  296.1 0.0 copy-done.3
  296.1 0.0 copy-done
  296.1 1.1 broadcast_select_fusion
  297.2 333.9 %backward.3 = bf16[15,72,2048]{2,1,0:T(8,128)(2,1)} custom-call(bf16[64,2048,256]{2,1,0:T(8,128)(2,1)} %get-tuple-element.74.at_hbm, bf16[1208,2048]{1,0:T(8,128)(2,1)} %gather_fusion, f32[16,72,128]{2,1,0:T(8,128)} %get-tuple-element.75.cc_ref, bf16[16,128,128]{2,1,0:T(8,128)(2,1)} %get-tuple-element.65.code_ref), custom_call_target="tpu_custom_call" | custom-call | tf_op jit(solution)/shard_map/cond/branch_0_fun/backward/pallas_call | solution.py:642
  631.1 18.7 %pairs.3 = f32[2048,2048]{1,0:T(8,128)} custom-call(s32[1]{0:T(128)} %bitcast.5.group_ref, bf16[16384,2048]{1,0:T(8,128)(2,1)} %get-tuple-element.142.a_hbm.a_ref, bf16[1080,2048]{1,0:T(8,128)(2,1)} %bitcast.45, bf16[1080,2048]{1,0:T(8,128)(2,1)} %bitcast.40), custom_call_target="tpu_custom_call" | custom-call | tf_op jit(solution)/shard_map/cond/branch_0_fun/pairs/pallas_call | solution.py:673
  (4 shorter events, 0.0 us)
Async XLA Ops:
  288.9 7.1 %copy-start.3 = (s32[128]{0:T(128)S(1)}, s32[128]{0:T(128)}, u32[]{:S(2)}) copy-start(s32[128]{0:T(128)} %get-tuple-element.69) | copy-start | bytes 1540 | tf_op jit(solution)/shard_map/cond
  289.0 7.1 %copy-start = (f32[128,2048]{1,0:T(8,128)S(1)}, f32[128,2048]{1,0:T(8,128)}, u32[]{:S(2)}) copy-start(f32[128,2048]{1,0:T(8,128)} %get-tuple-element.70) | copy-start | bytes 3145732 | tf_op jit(solution)/shard_map/cond
where the time goes:
time: 651 us; the launch traced here: 650 us
  Pallas kernels  622 us (96%)
  local copies, waits for them, and re-layouts  24.6 us (4%)
    pallas_call x1, Pallas kernels, _backward(): pl.pallas_call(functools.partial(_bwd_kernel, n, steps, rows, nbuf), out_...  334 us
    pallas_call x1, Pallas kernels, _forward(): pl.pallas_call(functools.partial(_fwd_kernel, n, steps, rows, nbuf), out_...  267 us
    pallas_call x1, Pallas kernels, _pairs(): pl.pallas_call(_pair_kernel, out_shape=jax.ShapeDtypeStruct((wide, wide),...  18.7 us
    gather x1, local copies, waits for them, and re-layouts, run(): e_rows = jnp.take(emit_loc, tokens, axis=1, mode='clip').T  17.4 us

commit v1 on v0

--- a/solution.py
+++ b/solution.py
@@ -20,8 +20,8 @@
     core = lax.rem(me, 2)
     chip = lax.div(me, 2)
     partner = chip * 2 + (1 - core)
-    right = lax.rem(me + 2, n)
-    left = lax.rem(me + n - 2, n)
+    right = lax.rem(partner + 2, n)
+    left = lax.rem(partner + n - 2, n)
     return me, chip, core, partner, right, left
 
 
@@ -68,8 +68,8 @@
         qq = jnp.where(j < 2, 2 * j + i, far)
         off = jnp.where(j < 2, 0, jnp.where(j >= 6, 2, jnp.where(i == 0, chips - 1, 1)))
         c = lax.rem(chip + off, chips)
-        k = jnp.where(cls == 0, core, 1 - core)
-        return (c * 2 + k) * 4 + qq
+        k = jnp.where((j >= 2) & (j < 6), cls == 0, cls != 0)
+        return (c * 2 + jnp.where(k, 1 - core, core)) * 4 + qq
 
     def a_part(b):
         return a_hbm.at[pl.ds(pl.multiple_of(b * part_w, part_w), part_w), :]
@@ -96,10 +96,11 @@
     def x_copy(s, q):
         return pltpu.make_async_copy(mine(me * 4 + q), x_hbm.at[s, :, pl.ds(q * part_w, part_w)], out_sem.at[q])
 
-    pieces, depth, size = at_hbm.shape[0], ta.shape[0], ta.shape[1]
+    pieces, size = at_hbm.shape[0], ta.shape[1]
+    fed, depth = ta.shape[0], tt.shape[0]
 
     def ta_copy(c):
-        slot = lax.rem(c, depth)
+        slot = lax.rem(c, fed)
         return pltpu.make_async_copy(a_hbm.at[pl.ds(pl.multiple_of(c * size, size), size), :], ta.at[slot], ta_sem.at[slot])
 
     def tt_copy(c):
@@ -115,12 +116,12 @@
                 tt_copy(c - depth).wait()
 
             slot = lax.rem(c, depth)
-            tt[slot] = ta[slot].T
+            tt[slot] = ta[lax.rem(c, fed)].T
             tt_copy(c).start()
 
-            @pl.when(c + depth < pieces)
-            def _():
-                ta_copy(c + depth).start()
+            @pl.when(c + fed < pieces)
+            def _():
+                ta_copy(c + fed).start()
 
             return 0
 
@@ -135,7 +136,7 @@
             resident(j, i).start()
         return 0
 
-    for c in range(depth):
+    for c in range(fed):
         ta_copy(jnp.int32(c)).start()
     for q in range(nbuf):
         stream(jnp.int32(q), q).start()
@@ -234,9 +235,6 @@
                         g[b, 0:rows, cols] = (fr[i, :, cols] / safe).astype(jnp.bfloat16)
                     relay(2, i).start()
                 pass_on(2)
-
-            @pl.when((h == 2) & (s + 2 < steps))
-            def _():
                 first_alphas(s + 1)
 
             @pl.when(s == 0)
@@ -436,14 +434,14 @@
             pltpu.VMEM((rows, wide), bf16),
             pltpu.VMEM((2, rows, part_w), f32),
             pltpu.VMEM((2, rows, part_w), f32),
-            pltpu.VMEM((4, part_w // 2, wide), bf16),
+            pltpu.VMEM((5, part_w // 2, wide), bf16),
             pltpu.VMEM((4, wide, part_w // 2), bf16),
             pltpu.VMEM((rows, LANES), f32),
             pltpu.VMEM((rows, LANES), f32),
             pltpu.VMEM((LANES, LANES), f32),
             pltpu.VMEM((8, LANES), f32),
             pltpu.VMEM((n, 8, LANES), f32),
-            dma((2,)), dma((nbuf,)), dma((2 * n,)), dma((5,)), dma((4,)), dma((4,)),
+            dma((2,)), dma((nbuf,)), dma((2 * n,)), dma((5,)), dma((5,)), dma((4,)),
             dma((n - 1,)), dma((n - 1,)),
             dma((12,)), dma((12,)), dma((2 * n,)), dma((2 * n,)),
         ],
@@ -471,7 +469,8 @@
         hh = jnp.where(p == 1, 1 - i, i)
         off = jnp.where(p == 0, 2, jnp.where(p == 3, 0, chips - 1 if i else 1))
         c = lax.rem(chip + off, chips)
-        k = 1 - core if cls else core
+        hop = (p == 1) | (p == 2)
+        k = jnp.where(hop, core if cls else 1 - core, 1 - core if cls else core)
         return (c * 2 + k) * 2 * per + hh * per + e
 
     def fetch(j, cls, i, slot, sem):

time: 651 us -> 639 us (0.982)
  Pallas kernels: 622 us -> 609 us
    pallas_call x1, Pallas kernels: 267 us -> 259 us  [_forward(): pl.pallas_call(functools.partial(_fwd_kernel, n, steps, rows, nbuf), out_...]
where the time goes in v1:
time: 639 us; the launch traced here: 637 us
  Pallas kernels  609 us (95%)
  local copies, waits for them, and re-layouts  24.4 us (4%)
    pallas_call x1, Pallas kernels, _backward(): pl.pallas_call(functools.partial(_bwd_kernel, n, steps, rows, nbuf), out_...  329 us
    pallas_call x1, Pallas kernels, _forward(): pl.pallas_call(functools.partial(_fwd_kernel, n, steps, rows, nbuf), out_...  259 us
    pallas_call x1, Pallas kernels, _pairs(): pl.pallas_call(_pair_kernel, out_shape=jax.ShapeDtypeStruct((wide, wide),...  18.7 us
    gather x1, local copies, waits for them, and re-layouts, run(): e_rows = jnp.take(emit_loc, tokens, axis=1, mode='clip').T  17.2 us

profile of v1, /device:TPU:112, one launch (start us, length us, event | category | flops | bytes accessed | tf_op | source)
XLA Modules:
  0.0 637.0 jit_solution(14306005751810981484)
XLA Ops:
  0.6 2.6 plan.1
  3.9 633.1 %conditional.1 = (f32[128]{0:T(128)}, f32[128,2048]{1,0:T(8,128)}, f32[2048,2048]{1,0:T(8,128)}) conditional(s32[]{:T(128)} %bitcast.27, (s32[16,128]{1,0:T(8,128)S(1)}, s32[128,16]{0,1:T(8,128)}, bf16[2048,10000]{0,1:T(8,128)(2,1)}, f32[2048]{0:T(1024)}, bf16[16384,2048]{1,0:T(8,128)(2,1)}, ...), branch_computations={%region_0.1_spmd, %region_1.2_spmd, %region_2.3_spmd} | conditional | flops 267520 | bytes 26265424 | solution.py:796
  3.9 0.7 slice_bitcast_fusion.1
  4.6 0.1 reshape.69
  4.6 0.1 pad_add_fusion
  4.7 17.2 %gather_fusion = bf16[1208,2048]{1,0:T(8,128)(2,1)} fusion(bf16[2048,10000]{0,1:T(8,128)(2,1)} %get-tuple-element.136, s32[2048]{0:T(1024)S(1)} %pad_clamp_fusion), kind=kCustom, calls=%fused_computation | custom fusion | bytes 9900768 | tf_op jit(solution)/shard_map/cond/branch_0_fun/jit(_take)/gather | solution.py:789
  21.9 258.9 %forward.3 = (f32[16,72,2048]{2,1,0:T(8,128)}, f32[128,2048]{1,0:T(8,128)}, bf16[15,72,2048]{2,1,0:T(8,128)(2,1)}, bf16[64,2048,256]{2,1,0:T(8,128)(2,1)}, f32[16,72,128]{2,1,0:T(8,128)}, /*index=5*/f32[8,128]{1,0:T(8,128)}) custom-call(bf16[16384,2048]{1,0:T(8,128)(2,1)} %get-tuple-element.142.a_hbm.a_ref, bf16[1208,2048]{1,0:T(8,128)(2,1)} %gather_fusion, ...), custom_call_target="tpu_custom_call" | custom-call | tf_op jit(solution)/shard_map/cond/branch_0_fun/forward/pallas_call | solution.py:415
  280.9 0.0 copy-start.3
  280.9 0.0 copy-start
  280.9 1.3 slice_bitcast_fusion
  282.2 0.7 convert_bitcast_fusion
  282.9 5.1 gather_fusion.1
  288.0 0.0 copy-done.3
  288.0 0.0 copy-done
  288.0 1.1 broadcast_select_fusion
  289.2 329.1 %backward.3 = bf16[15,72,2048]{2,1,0:T(8,128)(2,1)} custom-call(bf16[64,2048,256]{2,1,0:T(8,128)(2,1)} %get-tuple-element.74.at_hbm, bf16[1208,2048]{1,0:T(8,128)(2,1)} %gather_fusion, f32[16,72,128]{2,1,0:T(8,128)} %get-tuple-element.75.cc_ref, bf16[16,128,128]{2,1,0:T(8,128)(2,1)} %get-tuple-element.65.code_ref), custom_call_target="tpu_custom_call" | custom-call | tf_op jit(solution)/shard_map/cond/branch_0_fun/backward/pallas_call | solution.py:641
  618.3 18.7 %pairs.3 = f32[2048,2048]{1,0:T(8,128)} custom-call(s32[1]{0:T(128)} %bitcast.5.group_ref, bf16[16384,2048]{1,0:T(8,128)(2,1)} %get-tuple-element.142.a_hbm.a_ref, bf16[1080,2048]{1,0:T(8,128)(2,1)} %bitcast.45, bf16[1080,2048]{1,0:T(8,128)(2,1)} %bitcast.40), custom_call_target="tpu_custom_call" | custom-call | tf_op jit(solution)/shard_map/cond/branch_0_fun/pairs/pallas_call | solution.py:672
  (4 shorter events, 0.0 us)
Async XLA Ops:
  280.9 7.1 %copy-start.3 = (s32[128]{0:T(128)S(1)}, s32[128]{0:T(128)}, u32[]{:S(2)}) copy-start(s32[128]{0:T(128)} %get-tuple-element.69) | copy-start | bytes 1540 | tf_op jit(solution)/shard_map/cond
  280.9 7.1 %copy-start = (f32[128,2048]{1,0:T(8,128)S(1)}, f32[128,2048]{1,0:T(8,128)}, u32[]{:S(2)}) copy-start(f32[128,2048]{1,0:T(8,128)} %get-tuple-element.70) | copy-start | bytes 3145732 | tf_op jit(solution)/shard_map/cond

commit v2 on v1

--- a/solution.py
+++ b/solution.py
@@ -50,7 +50,7 @@
     return jnp.dot(x, y, preferred_element_type=jnp.float32)
 
 
-def _fwd_kernel(n, steps, rows, nbuf, a_hbm, e_hbm, pi_ref, code_ref, sid_ref, info_ref, al_hbm, a0_hbm, x_hbm, at_hbm, cc_ref, ll_ref,
+def _fwd_kernel(n, steps, rows, nbuf, a_hbm, e_hbm, pi_ref, code_ref, sid_ref, info_ref, al_hbm, x_hbm, at_hbm, cc_ref, ll_ref,
                 g, w, u, al, ebuf, a0b, xi, fs, fr, ta, tt, safe_ref, lacc, tbuf, cs_send, cs_recv,
                 e_sem, w_sem, r_sem, out_sem, ta_sem, tt_sem, cs_ss, cs_rs, ici_ss, ici_rs, dd_ss, dd_rs):
     me, chip, core, partner, right, left = _place(n)
@@ -88,7 +88,7 @@
         return e_rows((s - 1) * rows, rows, ebuf.at[lax.rem(s, 2)], e_sem.at[lax.rem(s, 2)])
 
     def al_copy(s):
-        return pltpu.make_async_copy(al, al_hbm.at[s], out_sem.at[4])
+        return pltpu.make_async_copy(al, al_hbm.at[pl.ds(pl.multiple_of((s - 1) * rows, 8), rows), :], out_sem.at[4])
 
     def mine(b):
         return g.at[b, pl.ds(0, rows), :]
@@ -125,7 +125,12 @@
 
             return 0
 
-        lax.fori_loop(lax.div((s - 1) * pieces, steps - 1), lax.div(s * pieces, steps - 1), one, 0)
+        @pl.when(s == 1)
+        def _():
+            for c in range(fed):
+                ta_copy(jnp.int32(c)).start()
+
+        lax.fori_loop(lax.div(jnp.maximum(s - 2, 0) * pieces, steps - 2), lax.div((s - 1) * pieces, steps - 2), one, 0)
 
     e0_copy = e_rows((steps - 1) * rows, seqs, a0b, e_sem.at[0])
     e0_copy.start()
@@ -136,8 +141,6 @@
             resident(j, i).start()
         return 0
 
-    for c in range(fed):
-        ta_copy(jnp.int32(c)).start()
     for q in range(nbuf):
         stream(jnp.int32(q), q).start()
     lax.fori_loop(0, 2, load, 0)
@@ -206,7 +209,7 @@
         lacc[...] += jnp.where(here, jnp.log(jnp.where(here, ccol, 1.0)), 0.0)
 
     def exchange(s, then):
-        own = [own_ring(3, i) for i in BOTH] + [dd(j, 0, i) for j in BOTH for i in BOTH]
+        own = [dd(j, 0, i) for j in BOTH for i in BOTH]
         own += [own_ring(j, i) for j in (4, 5) for i in BOTH]
         for cp in own:
             cp.start()
@@ -297,7 +300,7 @@
                 relay(j, i).wait_send()
             for j in range(2, 8):
                 dd(j, 0, i).wait_send()
-        for cp in own:
+        for cp in own + [own_ring(3, i) for i in BOTH]:
             cp.wait_send()
 
     def keep(s):
@@ -326,11 +329,13 @@
         return 0
 
     lax.fori_loop(0, wide // LANES, first_alpha, 0)
-    a0_copy = pltpu.make_async_copy(a0f, a0_hbm, e_sem.at[0])
+    a0_copy = pltpu.make_async_copy(a0f, al_hbm.at[pl.ds((steps - 1) * rows, seqs), :], e_sem.at[0])
     a0_copy.start()
     first_alphas(0)
     for q, cols in enumerate(_spans(wide, part_w)):
         g[me * 4 + q, 0:rows, :] = xi[:, cols]
+    for i in BOTH:
+        own_ring(3, i).start()
     safe_ref[...] = jnp.ones_like(safe_ref)
     for i in BOTH:
         fs[i] = xi[:, 2 * i * part_w:(2 * i + 1) * part_w].astype(jnp.float32)
@@ -385,13 +390,19 @@
         cc_ref[s] = ccol
         safe = jnp.where(live, ccol, 1.0)
         safe_ref[...] = jnp.where(starts, 1.0, safe)
-        for q, block in enumerate(_spans(wide, part_w)):
+        blocks = _spans(wide, part_w)
+        for q in (1, 3, 0, 2):
             for cols in _spans(part_w):
-                src = slice(block.start + cols.start, block.start + cols.stop)
+                src = slice(blocks[q].start + cols.start, blocks[q].start + cols.stop)
                 alpha = jnp.where(live, al[:, src] / safe, 0.0)
                 al[:, src] = alpha
                 x = jnp.where(starts, xi[:, src].astype(jnp.float32), alpha)
                 g[me * 4 + q, 0:rows, cols] = x.astype(jnp.bfloat16)
+
+            if q % 2:
+                @pl.when(s + 1 < steps)
+                def _():
+                    own_ring(3, q // 2).start()
 
         al_copy(s).start()
         return 0
@@ -415,15 +426,14 @@
     return pl.pallas_call(
         functools.partial(_fwd_kernel, n, steps, rows, nbuf),
         out_shape=(
-            jax.ShapeDtypeStruct((steps, rows, wide), f32),
-            jax.ShapeDtypeStruct((seqs, wide), f32),
+            jax.ShapeDtypeStruct(((steps - 1) * rows + seqs, wide), f32),
             jax.ShapeDtypeStruct((steps - 1, rows, wide), bf16),
             jax.ShapeDtypeStruct((2 * a_loc.shape[0] // part_w, wide, part_w // 2), bf16),
             jax.ShapeDtypeStruct((steps, rows, LANES), f32),
             jax.ShapeDtypeStruct((8, LANES), f32),
         ),
         in_specs=[ANY, ANY, VMEM, VMEM, VMEM, VMEM],
-        out_specs=(ANY, ANY, ANY, ANY, VMEM, VMEM),
+        out_specs=(ANY, ANY, ANY, VMEM, VMEM),
         scratch_shapes=[
             pltpu.VMEM((4 * n, full, part_w), bf16),
             pltpu.VMEM((2 * n + nbuf, part_w, wide), bf16),
@@ -728,7 +738,8 @@
     info_ref[0:1, :] = slot
     info_ref[1:2, :] = begin
     info_ref[2:3, :] = end
-    info_ref[3:4, :] = end * slots + slot
+    order = jax.lax.broadcasted_iota(jnp.int32, length.shape, 1).astype(f32)
+    info_ref[3:4, :] = jnp.where(length < 1.5, (steps - 1) * slots + order, (end - 1) * slots + slot)
 
     double = total(jnp.where((spread(slot).T == spread(slot)) & (up != across), 1.0, 0.0))
     shadowed = opens & (length < 1.5) & (double > 0.5)
@@ -787,11 +798,10 @@
             rows = options[k]
             tokens = jnp.concatenate([look[1:, 0:rows].reshape(-1), tokens_loc[:, 0]])
             e_rows = jnp.take(emit_loc, tokens, axis=1, mode='clip').T
-            al, a0, xs, at_loc, ccol, ll = _forward(n, 2 * k, rows, trans_loc, e_rows, init_loc[None, :], code, sid, info)
+            al, xs, at_loc, ccol, ll = _forward(n, 2 * k, rows, trans_loc, e_rows, init_loc[None, :], code, sid, info)
             ws = _backward(n, 2 * k + 1, at_loc, e_rows, ccol, code)
             counts = _pairs(group, trans_loc, xs.reshape(-1, wide), ws.reshape(-1, wide))
-            last = jnp.take(al.reshape(steps * rows, wide), info[3].astype(jnp.int32), axis=0, mode='clip')
-            return ll[0], jnp.where((lengths_loc == 1)[:, None], a0, last), counts
+            return ll[0], jnp.take(al, info[3].astype(jnp.int32), axis=0, mode='clip'), counts
 
         return lax.switch(pick[0, 0], [functools.partial(run, k) for k in range(len(options))])
 

time: 639 us -> 637 us (level)
  no operation moved by 1% of the time
where the time goes in v2:
time: 637 us; the launch traced here: 636 us
  Pallas kernels  607 us (95%)
  local copies, waits for them, and re-layouts  26.8 us (4%)
    pallas_call x1, Pallas kernels, _backward(): pl.pallas_call(functools.partial(_bwd_kernel, n, steps, rows, nbuf), out_...  329 us
    pallas_call x1, Pallas kernels, _forward(): pl.pallas_call(functools.partial(_fwd_kernel, n, steps, rows, nbuf), out_...  256 us
    pallas_call x1, Pallas kernels, _pairs(): pl.pallas_call(_pair_kernel, out_shape=jax.ShapeDtypeStruct((wide, wide),...  18.7 us
    gather x1, local copies, waits for them, and re-layouts, run(): e_rows = jnp.take(emit_loc, tokens, axis=1, mode='clip').T  18.7 us

profile of v2, /device:TPU:112, one launch (start us, length us, event | category | flops | bytes accessed | tf_op | source)
XLA Modules:
  0.0 635.7 jit_solution(11820452633467744195)
XLA Ops:
  0.6 2.6 plan.1
  3.8 631.8 %conditional.1 = (f32[128]{0:T(128)}, f32[128,2048]{1,0:T(8,128)}, f32[2048,2048]{1,0:T(8,128)}) conditional(s32[]{:T(128)} %bitcast.24, (s32[16,128]{1,0:T(8,128)S(1)}, s32[128,16]{0,1:T(8,128)}, bf16[2048,10000]{0,1:T(8,128)(2,1)}, f32[2048]{0:T(1024)}, bf16[16384,2048]{1,0:T(8,128)(2,1)}, ...), branch_computations={%region_0.1_spmd, %region_1.2_spmd, %region_2.3_spmd} | conditional | flops 5248 | bytes 18922520 | solution.py:806
  3.9 0.7 slice_bitcast_fusion.1
  4.5 0.1 reshape.60
  4.6 0.1 pad_add_fusion
  4.7 18.7 %gather_fusion = bf16[1208,2048]{1,0:T(8,128)(2,1)} fusion(bf16[2048,10000]{0,1:T(8,128)(2,1)} %get-tuple-element.124, s32[2048]{0:T(1024)S(1)} %pad_clamp_fusion), kind=kCustom, calls=%fused_computation | custom fusion | bytes 9900768 | tf_op jit(solution)/shard_map/cond/branch_0_fun/jit(_take)/gather | solution.py:800
  23.4 256.4 %forward.3 = (f32[1208,2048]{1,0:T(8,128)}, bf16[15,72,2048]{2,1,0:T(8,128)(2,1)}, bf16[64,2048,256]{2,1,0:T(8,128)(2,1)}, f32[16,72,128]{2,1,0:T(8,128)}, f32[8,128]{1,0:T(8,128)}) custom-call(bf16[16384,2048]{1,0:T(8,128)(2,1)} %get-tuple-element.130.a_hbm.a_ref, bf16[1208,2048]{1,0:T(8,128)(2,1)} %gather_fusion, f32[1,2048]{1,0:T(1,128)} %bitcast.41, ...), custom_call_target="tpu_custom_call" | custom-call | tf_op jit(solution)/shard_map/cond/branch_0_fun/forward/pallas_call | solution.py:426
  279.7 1.2 slice_bitcast_fusion
  280.9 0.7 convert_bitcast_fusion
  281.6 6.2 gather_fusion.1
  287.8 329.1 %backward.3 = bf16[15,72,2048]{2,1,0:T(8,128)(2,1)} custom-call(bf16[64,2048,256]{2,1,0:T(8,128)(2,1)} %get-tuple-element.66.at_hbm, bf16[1208,2048]{1,0:T(8,128)(2,1)} %gather_fusion, f32[16,72,128]{2,1,0:T(8,128)} %get-tuple-element.67.cc_ref, bf16[16,128,128]{2,1,0:T(8,128)(2,1)} %get-tuple-element.59.code_ref), custom_call_target="tpu_custom_call" | custom-call | tf_op jit(solution)/shard_map/cond/branch_0_fun/backward/pallas_call | solution.py:651
  617.0 18.7 %pairs.3 = f32[2048,2048]{1,0:T(8,128)} custom-call(s32[1]{0:T(128)} %bitcast.4.group_ref, bf16[16384,2048]{1,0:T(8,128)(2,1)} %get-tuple-element.130.a_hbm.a_ref, bf16[1080,2048]{1,0:T(8,128)(2,1)} %bitcast.40, bf16[1080,2048]{1,0:T(8,128)(2,1)} %bitcast.37), custom_call_target="tpu_custom_call" | custom-call | tf_op jit(solution)/shard_map/cond/branch_0_fun/pairs/pallas_call | solution.py:682
  (3 shorter events, 0.0 us)

commit v3 on v2

--- a/solution.py
+++ b/solution.py
@@ -738,8 +738,6 @@
     info_ref[0:1, :] = slot
     info_ref[1:2, :] = begin
     info_ref[2:3, :] = end
-    order = jax.lax.broadcasted_iota(jnp.int32, length.shape, 1).astype(f32)
-    info_ref[3:4, :] = jnp.where(length < 1.5, (steps - 1) * slots + order, (end - 1) * slots + slot)
 
     double = total(jnp.where((spread(slot).T == spread(slot)) & (up != across), 1.0, 0.0))
     shadowed = opens & (length < 1.5) & (double > 0.5)
@@ -793,6 +791,7 @@
         group = lax.axis_index('states').astype(jnp.int32)[None]
         options = (seqs * 9 // 16, seqs * 5 // 8, seqs)
         code, sid, look, info, pick = _plan(options, lengths_loc, tokens_loc.T)
+        branch = lax.pmax(pick[0, 0], 'seqs')
 
         def run(k):
             rows = options[k]
@@ -801,8 +800,11 @@
             al, xs, at_loc, ccol, ll = _forward(n, 2 * k, rows, trans_loc, e_rows, init_loc[None, :], code, sid, info)
             ws = _backward(n, 2 * k + 1, at_loc, e_rows, ccol, code)
             counts = _pairs(group, trans_loc, xs.reshape(-1, wide), ws.reshape(-1, wide))
-            return ll[0], jnp.take(al, info[3].astype(jnp.int32), axis=0, mode='clip'), counts
-
-        return lax.switch(pick[0, 0], [functools.partial(run, k) for k in range(len(options))])
+            slot, end = info[0].astype(jnp.int32), info[2].astype(jnp.int32)
+            alone = (steps - 1) * rows + jnp.arange(seqs, dtype=jnp.int32)
+            where = jnp.where(lengths_loc == 1, alone, (end - 1) * rows + slot)
+            return ll[0], jnp.take(al, where, axis=0, mode='clip'), counts
+
+        return lax.switch(branch, [functools.partial(run, k) for k in range(len(options))])
 
     return jax.shard_map(local_run, mesh=mesh, in_specs=(P(None, 'states'), P('states', None), P('states'), P('seqs', None), P('seqs')), out_specs=(P('seqs'), P('seqs', 'states'), P(('seqs', 'states'), None)), check_vma=False)

time: 637 us -> 640 us (level)
  no operation moved by 1% of the time
where the time goes in v3:
time: 640 us; the launch traced here: 639 us
  Pallas kernels  606 us (95%)
  local copies, waits for them, and re-layouts  25.4 us (4%)
    pallas_call x1, Pallas kernels, _backward(): pl.pallas_call(functools.partial(_bwd_kernel, n, steps, rows, nbuf), out_...  329 us
    pallas_call x1, Pallas kernels, _forward(): pl.pallas_call(functools.partial(_fwd_kernel, n, steps, rows, nbuf), out_...  256 us
    pallas_call x1, Pallas kernels, _pairs(): pl.pallas_call(_pair_kernel, out_shape=jax.ShapeDtypeStruct((wide, wide),...  18.7 us
    gather x1, local copies, waits for them, and re-layouts, run(): e_rows = jnp.take(emit_loc, tokens, axis=1, mode='clip').T  17.2 us

profile of v3, /device:TPU:112, one launch (start us, length us, event | category | flops | bytes accessed | tf_op | source)
XLA Modules:
  0.0 639.2 jit_solution(9804188066070947338)
XLA Ops:
  0.6 2.6 plan.1
  3.2 5.8 pmax.7
  9.6 629.6 %conditional.1 = (f32[128]{0:T(128)}, f32[128,2048]{1,0:T(8,128)}, f32[2048,2048]{1,0:T(8,128)}) conditional(s32[]{:T(128)} %clamp.3, (s32[16,128]{1,0:T(8,128)S(1)}, s32[128,16]{0,1:T(8,128)}, bf16[2048,10000]{0,1:T(8,128)(2,1)}, f32[2048]{0:T(1024)}, bf16[16384,2048]{1,0:T(8,128)(2,1)}, /*index=5*/bf16[16,128,128]{2,1,0:T(8,128)(2,1)}, ...), branch_computations={%region_1.2_spmd, %region_2.3_spmd, %region_3.4_spmd} | conditional | flops 6144 | bytes 18923544 | solution.py:808
  9.6 0.7 slice_bitcast_fusion.1
  10.3 0.1 reshape.45
  10.4 0.1 pad_add_fusion
  10.5 17.2 %gather_fusion = bf16[1208,2048]{1,0:T(8,128)(2,1)} fusion(bf16[2048,10000]{0,1:T(8,128)(2,1)} %get-tuple-element.133, s32[2048]{0:T(1024)S(1)} %pad_clamp_fusion), kind=kCustom, calls=%fused_computation | custom fusion | bytes 9900768 | tf_op jit(solution)/shard_map/cond/branch_0_fun/jit(_take)/gather | solution.py:799
  27.7 255.6 %forward.3 = (f32[1208,2048]{1,0:T(8,128)}, bf16[15,72,2048]{2,1,0:T(8,128)(2,1)}, bf16[64,2048,256]{2,1,0:T(8,128)(2,1)}, f32[16,72,128]{2,1,0:T(8,128)}, f32[8,128]{1,0:T(8,128)}) custom-call(bf16[16384,2048]{1,0:T(8,128)(2,1)} %get-tuple-element.139.a_hbm.a_ref, bf16[1208,2048]{1,0:T(8,128)(2,1)} %gather_fusion, f32[1,2048]{1,0:T(1,128)} %bitcast.41, ...), custom_call_target="tpu_custom_call" | custom-call | tf_op jit(solution)/shard_map/cond/branch_0_fun/forward/pallas_call | solution.py:426
  283.3 1.2 slice_bitcast_fusion
  284.5 0.8 compare_select_fusion
  285.3 6.2 gather_fusion.1
  291.5 329.1 %backward.3 = bf16[15,72,2048]{2,1,0:T(8,128)(2,1)} custom-call(bf16[64,2048,256]{2,1,0:T(8,128)(2,1)} %get-tuple-element.73.at_hbm, bf16[1208,2048]{1,0:T(8,128)(2,1)} %gather_fusion, f32[16,72,128]{2,1,0:T(8,128)} %get-tuple-element.74.cc_ref, bf16[16,128,128]{2,1,0:T(8,128)(2,1)} %get-tuple-element.65.code_ref), custom_call_target="tpu_custom_call" | custom-call | tf_op jit(solution)/shard_map/cond/branch_0_fun/backward/pallas_call | solution.py:651
  620.6 18.7 %pairs.3 = f32[2048,2048]{1,0:T(8,128)} custom-call(s32[1]{0:T(128)} %bitcast.4.group_ref, bf16[16384,2048]{1,0:T(8,128)(2,1)} %get-tuple-element.139.a_hbm.a_ref, bf16[1080,2048]{1,0:T(8,128)(2,1)} %bitcast.40, bf16[1080,2048]{1,0:T(8,128)(2,1)} %bitcast.37), custom_call_target="tpu_custom_call" | custom-call | tf_op jit(solution)/shard_map/cond/branch_0_fun/pairs/pallas_call | solution.py:682
  (3 shorter events, 0.0 us)

commit v4 on v2

--- a/solution.py
+++ b/solution.py
@@ -677,7 +677,7 @@
 
 def _pairs(group, a_loc, xs, ws):
     depth, wide = ws.shape
-    size = wide // 8
+    size = wide // (4 if 2 * depth < wide + LANES else 16)
     tiles = wide // size
     return pl.pallas_call(
         _pair_kernel,

time: 637 us -> 634 us (level)
  no operation moved by 1% of the time
where the time goes in v4:
time: 634 us
  Pallas kernels  606 us (96%)
  local copies, waits for them, and re-layouts  26.2 us (4%)
    pallas_call x1, Pallas kernels, _backward(): pl.pallas_call(functools.partial(_bwd_kernel, n, steps, rows, nbuf), out_...  329 us
    pallas_call x1, Pallas kernels, _forward(): pl.pallas_call(functools.partial(_fwd_kernel, n, steps, rows, nbuf), out_...  256 us
    gather x1, local copies, waits for them, and re-layouts, run(): e_rows = jnp.take(emit_loc, tokens, axis=1, mode='clip').T  18.1 us
    pallas_call x1, Pallas kernels, _pairs(): pl.pallas_call(_pair_kernel, out_shape=jax.ShapeDtypeStruct((wide, wide),...  17.5 us

profile of v4, /device:TPU:112, one launch (start us, length us, event | category | flops | bytes accessed | tf_op | source)
XLA Modules:
  0.0 633.9 jit_solution(9761780687637511083)
XLA Ops:
  0.6 2.6 plan.1
  3.8 630.0 %conditional.1 = (f32[128]{0:T(128)}, f32[128,2048]{1,0:T(8,128)}, f32[2048,2048]{1,0:T(8,128)}) conditional(s32[]{:T(128)} %bitcast.24, (s32[16,128]{1,0:T(8,128)S(1)}, s32[128,16]{0,1:T(8,128)}, bf16[2048,10000]{0,1:T(8,128)(2,1)}, f32[2048]{0:T(1024)}, bf16[16384,2048]{1,0:T(8,128)(2,1)}, ...), branch_computations={%region_0.1_spmd, %region_1.2_spmd, %region_2.3_spmd} | conditional | flops 5248 | bytes 18922520 | solution.py:806
  3.9 0.7 slice_bitcast_fusion.1
  4.5 0.1 reshape.60
  4.6 0.1 pad_add_fusion
  4.7 18.1 %gather_fusion = bf16[1208,2048]{1,0:T(8,128)(2,1)} fusion(bf16[2048,10000]{0,1:T(8,128)(2,1)} %get-tuple-element.124, s32[2048]{0:T(1024)S(1)} %pad_clamp_fusion), kind=kCustom, calls=%fused_computation | custom fusion | bytes 9900768 | tf_op jit(solution)/shard_map/cond/branch_0_fun/jit(_take)/gather | solution.py:800
  22.8 256.4 %forward.3 = (f32[1208,2048]{1,0:T(8,128)}, bf16[15,72,2048]{2,1,0:T(8,128)(2,1)}, bf16[64,2048,256]{2,1,0:T(8,128)(2,1)}, f32[16,72,128]{2,1,0:T(8,128)}, f32[8,128]{1,0:T(8,128)}) custom-call(bf16[16384,2048]{1,0:T(8,128)(2,1)} %get-tuple-element.130.a_hbm.a_ref, bf16[1208,2048]{1,0:T(8,128)(2,1)} %gather_fusion, f32[1,2048]{1,0:T(1,128)} %bitcast.41, ...), custom_call_target="tpu_custom_call" | custom-call | tf_op jit(solution)/shard_map/cond/branch_0_fun/forward/pallas_call | solution.py:426
  279.2 1.2 slice_bitcast_fusion
  280.4 0.7 convert_bitcast_fusion
  281.1 6.2 gather_fusion.1
  287.2 329.1 %backward.3 = bf16[15,72,2048]{2,1,0:T(8,128)(2,1)} custom-call(bf16[64,2048,256]{2,1,0:T(8,128)(2,1)} %get-tuple-element.66.at_hbm, bf16[1208,2048]{1,0:T(8,128)(2,1)} %gather_fusion, f32[16,72,128]{2,1,0:T(8,128)} %get-tuple-element.67.cc_ref, bf16[16,128,128]{2,1,0:T(8,128)(2,1)} %get-tuple-element.59.code_ref), custom_call_target="tpu_custom_call" | custom-call | tf_op jit(solution)/shard_map/cond/branch_0_fun/backward/pallas_call | solution.py:651
  616.3 17.5 %pairs.3 = f32[2048,2048]{1,0:T(8,128)} custom-call(s32[1]{0:T(128)} %bitcast.4.group_ref, bf16[16384,2048]{1,0:T(8,128)(2,1)} %get-tuple-element.130.a_hbm.a_ref, bf16[1080,2048]{1,0:T(8,128)(2,1)} %bitcast.40, bf16[1080,2048]{1,0:T(8,128)(2,1)} %bitcast.37), custom_call_target="tpu_custom_call" | custom-call | tf_op jit(solution)/shard_map/cond/branch_0_fun/pairs/pallas_call | solution.py:682
  (3 shorter events, 0.0 us)
